TPU v7x, 32 devices: a whole 2x2x4 slice. The times are simulated.
32 devices in a mesh: row: 4 (over y, x), col: 8 (over z, core).
Axes of the slice: x: 2, y: 2, z: 4, core: 2. Of those that a mesh axis runs over, the one named last changes fastest.
Arguments:
- patches: bfloat16 [32, 128, 768], P('row', 'col'), may hold values from -6 to 6
- w_patch: bfloat16 [768, 6144], replicated, may hold values from -0.21875 to 0.21875
- patch_bias: bfloat16 [6144], replicated, may hold values from -5 to 5
- ln_gain: bfloat16 [6144], replicated, may hold values from 0.5 to 1.5
- w_qkv: bfloat16 [6144, 3, 48, 128], P(None, None, 'col'), may hold values from -1 to 1
- qk_gain: float32 [2, 48, 128], P(None, 'col'), may hold values from 0 to 6, as said below
- w_out: bfloat16 [48, 128, 6144], P('col', None, 'row'), may hold values from -0.078125 to 0.078125
Outputs:
- attn_branch: bfloat16 [4096, 6144], P(('row', 'col'))
Inputs may be any that keep to these rules, and one draw needn't show every extreme that they name: `qk_gain`: positive gains.
All inputs are finite; a program needn't handle non-finite values.
Results may differ from a plain program's by a relative error of at most 0.015.
Values may be sent and summed in bfloat16 or wider, within the bound.
A program may use at most 320 MiB of HBM per device.

v0:
```python
import math
import jax
import jax.numpy as jnp
from jax import lax
from jax.sharding import PartitionSpec as P

NORM_EPS = 1e-06


def sincos_table(row_ids, col_ids, model_width):
    quarter = model_width // 4
    frequency = 1.0 / 10000.0 ** (jnp.arange(quarter, dtype=jnp.float32) / quarter)
    row_angle = row_ids.astype(jnp.float32)[:, None] * frequency[None, :]
    col_angle = col_ids.astype(jnp.float32)[:, None] * frequency[None, :]
    return jnp.concatenate(
        [jnp.sin(row_angle), jnp.cos(row_angle), jnp.sin(col_angle), jnp.cos(col_angle)], axis=1
    )


def layer_norm(values, gain_row):
    mean_val = jnp.mean(values, axis=-1, keepdims=True)
    centered = values - mean_val
    variance = jnp.mean(centered * centered, axis=-1, keepdims=True)
    return centered * lax.rsqrt(variance + NORM_EPS) * gain_row


def local(patches, w_patch, patch_bias, ln_gain, w_qkv, qk_gain, w_out):
    tile_rows, tile_cols, pixel_width = patches.shape
    model_width = w_patch.shape[1]
    heads_here = w_qkv.shape[2]
    head_size = w_qkv.shape[3]
    col_count = lax.axis_size("col")
    block_tokens = tile_rows * tile_cols * col_count
    row_anchor = lax.axis_index("row") * tile_rows
    qkv_matrix = w_qkv.reshape(model_width, 3 * heads_here * head_size)
    bias_row = patch_bias.astype(jnp.float32)[None, :]
    gain_row = ln_gain.astype(jnp.float32)
    pixels = lax.all_gather(patches, "col", axis=1, tiled=True)
    piece_cols = pixels.shape[1]
    local_rows = jnp.repeat(jnp.arange(tile_rows, dtype=jnp.int32), piece_cols)
    local_cols = jnp.tile(jnp.arange(piece_cols, dtype=jnp.int32), tile_rows)
    flat_pixels = pixels.reshape(tile_rows * piece_cols, pixel_width)
    embedded = jnp.dot(flat_pixels, w_patch, preferred_element_type=jnp.float32) + bias_row
    embedded = embedded + sincos_table(row_anchor + local_rows, local_cols, model_width)
    normed = layer_norm(embedded, gain_row).astype(jnp.bfloat16)
    normed_piece = normed.reshape(tile_rows, piece_cols, model_width)
    project_piece_cols = normed_piece.shape[1]
    flat_normed = normed_piece.reshape(tile_rows * project_piece_cols, model_width)
    projected = jnp.dot(flat_normed, qkv_matrix, preferred_element_type=jnp.float32)
    projected = projected.reshape(tile_rows, project_piece_cols, 3 * heads_here * head_size)
    projected = projected.reshape(block_tokens, 3, heads_here, head_size)
    queries = layer_norm(projected[:, 0], qk_gain[0]).astype(jnp.bfloat16)
    keys_here = layer_norm(projected[:, 1], qk_gain[1]).astype(jnp.bfloat16)
    values_here = projected[:, 2].astype(jnp.bfloat16)
    query_heads = queries.transpose(1, 0, 2)
    scale_factor = 1.0 / math.sqrt(head_size)
    start_state = (
        jnp.full((heads_here, block_tokens), -1e30, jnp.float32),
        jnp.zeros((heads_here, block_tokens), jnp.float32),
        jnp.zeros((heads_here, block_tokens, head_size), jnp.float32),
    )
    key_piece = lax.all_gather(keys_here, "row", axis=0, tiled=True)
    value_piece = lax.all_gather(values_here, "row", axis=0, tiled=True)
    piece_len = key_piece.shape[0]
    key_block = math.gcd(piece_len, 1024)
    block_count = piece_len // key_block
    key_blocks = key_piece.reshape(block_count, key_block, heads_here, head_size)
    value_blocks = value_piece.reshape(block_count, key_block, heads_here, head_size)

    def step_block(state, block_args):
        run_peak, run_total, run_acc = state
        block_keys, block_values = block_args
        scores = (
            jnp.einsum("hqd,khd->hqk", query_heads, block_keys, preferred_element_type=jnp.float32)
            * scale_factor
        )
        new_peak = jnp.maximum(run_peak, jnp.max(scores, axis=2))
        rescale = jnp.exp(run_peak - new_peak)
        exponent = jnp.exp(scores - new_peak[:, :, None])
        new_total = run_total * rescale + jnp.sum(exponent, axis=2)
        weighted = jnp.einsum(
            "hqk,khd->hqd",
            exponent.astype(jnp.bfloat16),
            block_values,
            preferred_element_type=jnp.float32,
        )
        new_acc = run_acc * rescale[:, :, None] + weighted
        return ((new_peak, new_total, new_acc), None)

    final_state, unused = lax.scan(step_block, start_state, (key_blocks, value_blocks))
    peak_all, total_all, acc_all = final_state
    context = (acc_all / total_all[:, :, None]).astype(jnp.bfloat16)
    context = context.transpose(1, 0, 2).reshape(block_tokens, heads_here * head_size)
    out_weight = lax.all_gather(w_out, "row", axis=2, tiled=True).reshape(
        heads_here * head_size, model_width
    )
    return lax.psum_scatter(
        jnp.dot(context, out_weight, preferred_element_type=jnp.float32).astype(jnp.bfloat16),
        "col",
        scatter_dimension=0,
        tiled=True,
    )


def solution(mesh):
    return jax.shard_map(
        local,
        mesh=mesh,
        in_specs=(
            P("row", "col", None),
            P(),
            P(),
            P(),
            P(None, None, "col", None),
            P(None, "col", None),
            P("col", None, "row"),
        ),
        out_specs=P(("row", "col"), None),
        check_vma=False,
    )
```

profile of v0, /device:TPU:0, one launch (start us, length us, event | category | flops | bytes accessed | tf_op | source)
XLA Modules:
  0.0 631.0 jit_solution(16349719539641851866)
XLA Ops:
  8.0 36.8 %copy.13 = bf16[6144,3,6,128]{0,3,2,1:T(8,128)(2,1)} copy(bf16[6144,3,6,128]{3,0,2,1:T(8,128)(2,1)} %param.13) | data formatting | bytes 56623104 | tf_op args[4]
  44.9 46.9 %multiply_sine_fusion.1 = (f32[1024,1536]{1,0:T(8,128)}, f32[1024,1536]{1,0:T(8,128)}, f32[1024,1536]{1,0:T(8,128)}, f32[1024,1536]{1,0:T(8,128)}) fusion(f32[1536]{0:T(1024)S(1)} %negate_power_fusion, f32[1024]{0:T(1024)S(1)} %get-tuple-element.118, f32[1024]{0:T(1024)S(1)} %get-tuple-element.117), kind=kLoop, calls=%fused_computation.35 | loop fusion | flops 3145728 | bytes 25180160 | tf_op jit(solution)/shard_map/sin | solution.py:16
  91.8 24.2 %fusion.29 = (f32[1024]{0:T(1024)S(1)}, f32[1024,6144]{1,0:T(8,128)}) fusion(f32[1024,1536]{1,0:T(8,128)} %get-tuple-element.111, f32[1024,1536]{1,0:T(8,128)} %get-tuple-element.112, f32[1024,1536]{1,0:T(8,128)} %get-tuple-element.108, f32[1024,1536]{1,0:T(8,128)} %get-tuple-element.107, f32[6144]{0:T(1024)S(1)} %convert_element_type.52, ...), kind=kOutput, calls=%fused_computation.60 | convolution fusion | flops 9701424128 | bytes 61370368 | tf_op jit(solution)/shard_map/dot_general | solution.py:43
  126.2 36.4 %fusion.19 = f32[1024,3,6,128]{0,3,2,1:T(8,128)S(1)} fusion(bf16[6144,3,6,128]{0,3,2,1:T(8,128)(2,1)} %copy.13, f32[1024,6144]{1,0:T(8,128)} %get-tuple-element.116, f32[6144]{0:T(1024)S(1)} %convert_element_type.57, f32[1024]{0:T(1024)S(1)} %add_rsqrt_fusion.2, f32[1024]{0:T(1024)S(1)} %broadcast_multiply_fusion.2), kind=kOutput, calls=%fused_computation.22 | convolution fusion | flops 29016195072 | bytes 62947328 | tf_op jit(solution)/shard_map/dot_general | solution.py:49
  173.3 67.7 %all-gather.8.cloned.1.call-done = bf16[4096,6,128]{0,2,1:T(8,128)(2,1)} async-done(((bf16[1024,6,128]{0,2,1:T(8,128)(2,1)}), bf16[4096,6,128]{0,2,1:T(8,128)(2,1)}) %all-gather.8.cloned.1.call-update) | async-done | bytes 6291472 | tf_op jit(solution)/shard_map/all_gather | solution.py:62
  241.0 11.3 %reshape.81 = bf16[4,1024,6,128]{1,0,3,2:T(4,128)(2,1)} reshape(bf16[4096,6,128]{0,2,1:T(8,128)(2,1)} %all-gather.8.cloned.1.call-done) | data formatting | bytes 12582912 | tf_op jit(solution)/shard_map/reshape | solution.py:67
  252.4 11.4 %copy.16 = bf16[4,1024,6,128]{3,1,2,0:T(8,128)(2,1)} copy(bf16[4,1024,6,128]{1,0,3,2:T(4,128)(2,1)} %reshape.81) | data formatting | bytes 12582912
  263.7 49.2 %all-gather.12.cloned.1.call-done = bf16[4096,1,6,128]{0,3,2,1:T(8,128)(2,1)} async-done(((bf16[1024,1,6,128]{0,3,2,1:T(8,128)(2,1)}), bf16[4096,1,6,128]{0,3,2,1:T(8,128)(2,1)}) %all-gather.12.cloned.1.call-update) | async-done | bytes 6291472 | tf_op jit(solution)/shard_map/all_gather | solution.py:63
  313.0 11.4 %reshape.82 = bf16[4,1024,6,128]{1,0,3,2:T(4,128)(2,1)} reshape(bf16[4096,1,6,128]{0,3,2,1:T(8,128)(2,1)} %all-gather.12.cloned.1.call-done) | data formatting | bytes 12582912 | tf_op jit(solution)/shard_map/reshape | solution.py:68
  324.4 11.3 %copy.18 = bf16[4,1024,6,128]{3,1,2,0:T(8,128)(2,1)} copy(bf16[4,1024,6,128]{1,0,3,2:T(4,128)(2,1)} %reshape.82) | data formatting | bytes 12582912
  335.7 143.7 %while.15 = (s32[]{:T(128)}, f32[6,1024]{1,0:T(8,128)S(1)}, f32[6,1024]{1,0:T(8,128)S(1)}, f32[6,1024,128]{2,1,0:T(8,128)}, bf16[4,1024,6,128]{3,1,2,0:T(8,128)(...) while((s32[]{:T(128)}, f32[6,1024]{1,0:T(8,128)S(1)}, ...), condition=%wide.region_9.10_spmd.clone, body=%wide.region_6.9_spmd.clone.sunk | while | flops 3273947136 | bytes 86901856 | solution.py:90
  335.7 11.5 %bitcast_reduce_fusion.2 = (f32[6,1024]{1,0:T(8,128)S(1)}, f32[6,1024,1024]{2,1,0:T(8,128)}) fusion(bf16[6,1024,128]{2,1,0:T(8,128)(2,1)S(1)} %get-tuple-element.195, bf16[4,1024,6,128]{3,1,2,0:T(8,128)(2,1)} %get-tuple-element.194, s32[]{:T(128)} %get-tuple-element.181), kind=kOutput, calls=%fused_computation.1.clone.1 | convolution fusion | flops 1623189504 | bytes 28336640 | tf_op jit(solution)/shard_map/while/body/eval_jaxpr/hqd,khd->hqk/dot_general | solution.py:74
  347.1 10.5 %fusion.43 = f32[6,1024]{1,0:T(8,128)S(1)} fusion(f32[6,1024,1024]{2,1,0:T(8,128)} %get-tuple-element.169, f32[6,1024]{1,0:T(8,128)S(1)} %select_maximum_fusion.2), kind=kLoop, calls=%fused_computation.4.clone.1 | loop fusion | flops 18868224 | bytes 25214976 | tf_op jit(solution)/shard_map/while/body/eval_jaxpr/reduce_sum | solution.py:80
  357.7 14.2 %fusion.45 = f32[6,1024,128]{2,1,0:T(8,128)} fusion(f32[6,1024,128]{2,1,0:T(8,128)} %get-tuple-element.184, f32[6,1024,1024]{2,1,0:T(8,128)} %get-tuple-element.169, f32[6,1024]{1,0:T(8,128)S(1)} %select_maximum_fusion.2, bf16[4,1024,6,128]{3,1,2,0:T(8,128)(2,1)} %get-tuple-element.196, s32[]{:T(128)} %get-tuple-element.181, ...), kind=kOutput, calls=%fused_computation.9.clone.1 | convolution fusion | flops 1631846400 | bytes 33079808 | tf_op jit(solution)/shard_map/while/body/eval_jaxpr/hqk,khd->hqd/dot_general | solution.py:81
  371.9 11.5 %bitcast_reduce_fusion.2 = (f32[6,1024]{1,0:T(8,128)S(1)}, f32[6,1024,1024]{2,1,0:T(8,128)}) fusion(bf16[6,1024,128]{2,1,0:T(8,128)(2,1)S(1)} %get-tuple-element.195, bf16[4,1024,6,128]{3,1,2,0:T(8,128)(2,1)} %get-tuple-element.194, s32[]{:T(128)} %get-tuple-element.181), kind=kOutput, calls=%fused_computation.1.clone.1 | convolution fusion | flops 1623189504 | bytes 28336640 | tf_op jit(solution)/shard_map/while/body/eval_jaxpr/hqd,khd->hqk/dot_general | solution.py:74
  383.4 10.5 %fusion.43 = f32[6,1024]{1,0:T(8,128)S(1)} fusion(f32[6,1024,1024]{2,1,0:T(8,128)} %get-tuple-element.169, f32[6,1024]{1,0:T(8,128)S(1)} %select_maximum_fusion.2), kind=kLoop, calls=%fused_computation.4.clone.1 | loop fusion | flops 18868224 | bytes 25214976 | tf_op jit(solution)/shard_map/while/body/eval_jaxpr/reduce_sum | solution.py:80
  394.0 13.7 %fusion.45 = f32[6,1024,128]{2,1,0:T(8,128)} fusion(f32[6,1024,128]{2,1,0:T(8,128)} %get-tuple-element.184, f32[6,1024,1024]{2,1,0:T(8,128)} %get-tuple-element.169, f32[6,1024]{1,0:T(8,128)S(1)} %select_maximum_fusion.2, bf16[4,1024,6,128]{3,1,2,0:T(8,128)(2,1)} %get-tuple-element.196, s32[]{:T(128)} %get-tuple-element.181, ...), kind=kOutput, calls=%fused_computation.9.clone.1 | convolution fusion | flops 1631846400 | bytes 33079808 | tf_op jit(solution)/shard_map/while/body/eval_jaxpr/hqk,khd->hqd/dot_general | solution.py:81
  407.8 11.5 %bitcast_reduce_fusion.2 = (f32[6,1024]{1,0:T(8,128)S(1)}, f32[6,1024,1024]{2,1,0:T(8,128)}) fusion(bf16[6,1024,128]{2,1,0:T(8,128)(2,1)S(1)} %get-tuple-element.195, bf16[4,1024,6,128]{3,1,2,0:T(8,128)(2,1)} %get-tuple-element.194, s32[]{:T(128)} %get-tuple-element.181), kind=kOutput, calls=%fused_computation.1.clone.1 | convolution fusion | flops 1623189504 | bytes 28336640 | tf_op jit(solution)/shard_map/while/body/eval_jaxpr/hqd,khd->hqk/dot_general | solution.py:74
  419.2 10.5 %fusion.43 = f32[6,1024]{1,0:T(8,128)S(1)} fusion(f32[6,1024,1024]{2,1,0:T(8,128)} %get-tuple-element.169, f32[6,1024]{1,0:T(8,128)S(1)} %select_maximum_fusion.2), kind=kLoop, calls=%fused_computation.4.clone.1 | loop fusion | flops 18868224 | bytes 25214976 | tf_op jit(solution)/shard_map/while/body/eval_jaxpr/reduce_sum | solution.py:80
  429.8 13.7 %fusion.45 = f32[6,1024,128]{2,1,0:T(8,128)} fusion(f32[6,1024,128]{2,1,0:T(8,128)} %get-tuple-element.184, f32[6,1024,1024]{2,1,0:T(8,128)} %get-tuple-element.169, f32[6,1024]{1,0:T(8,128)S(1)} %select_maximum_fusion.2, bf16[4,1024,6,128]{3,1,2,0:T(8,128)(2,1)} %get-tuple-element.196, s32[]{:T(128)} %get-tuple-element.181, ...), kind=kOutput, calls=%fused_computation.9.clone.1 | convolution fusion | flops 1631846400 | bytes 33079808 | tf_op jit(solution)/shard_map/while/body/eval_jaxpr/hqk,khd->hqd/dot_general | solution.py:81
  443.6 11.5 %bitcast_reduce_fusion.2 = (f32[6,1024]{1,0:T(8,128)S(1)}, f32[6,1024,1024]{2,1,0:T(8,128)}) fusion(bf16[6,1024,128]{2,1,0:T(8,128)(2,1)S(1)} %get-tuple-element.195, bf16[4,1024,6,128]{3,1,2,0:T(8,128)(2,1)} %get-tuple-element.194, s32[]{:T(128)} %get-tuple-element.181), kind=kOutput, calls=%fused_computation.1.clone.1 | convolution fusion | flops 1623189504 | bytes 28336640 | tf_op jit(solution)/shard_map/while/body/eval_jaxpr/hqd,khd->hqk/dot_general | solution.py:74
  465.6 13.7 %fusion.45 = f32[6,1024,128]{2,1,0:T(8,128)} fusion(f32[6,1024,128]{2,1,0:T(8,128)} %get-tuple-element.184, f32[6,1024,1024]{2,1,0:T(8,128)} %get-tuple-element.169, f32[6,1024]{1,0:T(8,128)S(1)} %select_maximum_fusion.2, bf16[4,1024,6,128]{3,1,2,0:T(8,128)(2,1)} %get-tuple-element.196, s32[]{:T(128)} %get-tuple-element.181, ...), kind=kOutput, calls=%fused_computation.9.clone.1 | convolution fusion | flops 1631846400 | bytes 33079808 | tf_op jit(solution)/shard_map/while/body/eval_jaxpr/hqk,khd->hqd/dot_general | solution.py:81
  479.4 15.5 %bitcast_convert_fusion = bf16[1024,6144]{1,0:T(8,128)(2,1)} fusion(bf16[6,128,6144]{2,1,0:T(8,128)(2,1)} %all-gather.10.cloned.1.call-done, f32[6,1024,128]{2,1,0:T(8,128)} %get-tuple-element.43, f32[6,1024]{1,0:T(8,128)S(1)} %get-tuple-element.44), kind=kOutput, calls=%fused_computation.25 | convolution fusion | flops 9671540736 | bytes 25190400 | tf_op jit(solution)/shard_map/dot_general | solution.py:98
  494.9 129.6 %reduce-scatter.2.cloned.1.call-done = bf16[128,6144]{1,0:T(8,128)(2,1)} async-done(((bf16[1024,6144]{1,0:T(8,128)(2,1)}), bf16[128,6144]{1,0:T(8,128)(2,1)}) %reduce-scatter.2.cloned.1.call-update) | async-done | bytes 1572880 | tf_op jit(solution)/shard_map/reduce_scatter | solution.py:97
  (52 shorter events, 33.0 us)
Async XLA Ops:
  6.5 85.3 %all-gather.6.cloned.1.call-start = ((), (), s32[]{:S(2)}) async-start(), calls=%async_computation.1 | async-start | bytes 1769472 | tf_op jit(solution)/shard_map/all_gather | solution.py:38
  7.3 233.8 %all-gather.8.cloned.1.call-start = ((), (), s32[]{:S(2)}) async-start(), calls=%async_computation.2 | async-start | bytes 7864320 | tf_op jit(solution)/shard_map/all_gather | solution.py:62
  8.0 36.8 %copy-start.1 = (bf16[6144]{0:T(1024)(128)(2,1)S(1)}, bf16[6144]{0:T(1024)(128)(2,1)}, u32[]{:S(2)}) copy-start(bf16[6144]{0:T(1024)(128)(2,1)} %param.12) | copy-start | bytes 36868
  8.0 36.8 %copy-start.2 = (f32[2,6,128]{2,0,1:T(2,128)S(1)}, f32[2,6,128]{2,0,1:T(2,128)}, u32[]{:S(2)}) copy-start(f32[2,6,128]{2,0,1:T(2,128)} %param.14) | copy-start | bytes 18436
  162.7 3.6 copy-start
  168.1 144.8 %all-gather.12.cloned.1.call-start = ((), (), s32[]{:S(2)}) async-start(), calls=%async_computation.5 | async-start | bytes 7864320 | tf_op jit(solution)/shard_map/all_gather | solution.py:63
  171.5 307.9 %all-gather.10.cloned.1.call-start = ((), (), s32[]{:S(2)}) async-start(), calls=%async_computation.3 | async-start | bytes 11796480 | tf_op jit(solution)/shard_map/all_gather | solution.py:94
  172.1 452.4 %reduce-scatter.2.cloned.1.call-start = ((), (), s32[]{:S(2)}) async-start(), calls=%async_computation.4 | async-start | bytes 14155776 | tf_op jit(solution)/shard_map/reduce_scatter | solution.py:97
Sparse Core Ops, SparseCore 0:
  8.9 27.9 all-gather.5
  168.2 72.7 all-gather.7
  242.9 70.0 all-gather.11
  314.7 96.2 all-gather.9
  495.0 129.3 reduce-scatter.1
where the time goes:
time: 634 us; the launch traced here: 631 us
  waiting for transfers between devices  248 us (39%)
  matrix products  177 us (28%)
  other arithmetic  104 us (16%)
  local copies, waits for them, and re-layouts  88.6 us (14%)
  between operations  13.3 us (2%)
    reduce_scatter x1, waiting for transfers between devices, local(): lax.psum_scatter(jnp.dot(context, out_weight, preferred_element_type=jnp....  130 us
    all_gather x1, waiting for transfers between devices, local(): key_piece = lax.all_gather(keys_here, 'row', axis=0, tiled=True)  67.7 us
    unnamed x10, local copies, waits for them, and re-layouts  62.5 us
    dot_general x4, matrix products, step_block(): jnp.einsum('hqk,khd->hqd', exponent.astype(jnp.bfloat16), block_values, p...  55.5 us
    all_gather x1, waiting for transfers between devices, local(): value_piece = lax.all_gather(values_here, 'row', axis=0, tiled=True)  49.2 us
    sin x1, other arithmetic, sincos_table(): jnp.sin(row_angle)  46.9 us
    dot_general x4, matrix products, step_block(): jnp.einsum('hqd,khd->hqk', query_heads, block_keys, preferred_element_typ...  45.9 us
    reduce_sum x4, other arithmetic, step_block(): new_total = run_total * rescale + jnp.sum(exponent, axis=2)  42.2 us
  transfers between devices with their start and end apart: 5, of which 3 were waited for; matrix products, arithmetic and copies ran while one was open for 44% of the time, Pallas kernels for 0%

commit v1 on v0

--- a/solution.py
+++ b/solution.py
@@ -5,6 +5,16 @@
 from jax.sharding import PartitionSpec as P
 
 NORM_EPS = 1e-06
+
+
+def around_the_ring(x, axis, dim):
+    devices = lax.axis_size(axis)
+    held, blocks = (x, [x])
+    for _ in range(devices - 1):
+        held = lax.ppermute(held, axis, [(i, (i + 1) % devices) for i in range(devices)])
+        blocks.insert(0, held)
+    line = jnp.concatenate(blocks, axis=dim)
+    return jnp.roll(line, (lax.axis_index(axis) + 1) * x.shape[dim], axis=dim)
 
 
 def sincos_table(row_ids, col_ids, model_width):
@@ -59,7 +69,7 @@
         jnp.zeros((heads_here, block_tokens), jnp.float32),
         jnp.zeros((heads_here, block_tokens, head_size), jnp.float32),
     )
-    key_piece = lax.all_gather(keys_here, "row", axis=0, tiled=True)
+    key_piece = around_the_ring(keys_here, "row", 0)
     value_piece = lax.all_gather(values_here, "row", axis=0, tiled=True)
     piece_len = key_piece.shape[0]
     key_block = math.gcd(piece_len, 1024)

time: 634 us -> 698 us (1.10)
  waiting for transfers between devices: 248 us -> 307 us
    ppermute x0 -> x3, waiting for transfers between devices: none -> 177 us  [around_the_ring(): lax.ppermute(held, axis, [(i, (i + 1) % devices) for i in range(devices)])]
    all_gather x1 -> x0, waiting for transfers between devices: 67.7 us -> none  [local(): key_piece = lax.all_gather(keys_here, 'row', axis=0, tiled=True)]
    all_gather x1, waiting for transfers between devices: 49.2 us -> 0.01 us  [local(): value_piece = lax.all_gather(values_here, 'row', axis=0, tiled=True)]
    dynamic_slice x0 -> x2, local copies, waits for them, and re-layouts: none -> 11.9 us  [around_the_ring(): return jnp.roll(line, (lax.axis_index(axis) + 1) * x.shape[dim], axis=dim)]
    reshape x1 -> x0, local copies, waits for them, and re-layouts: 11.3 us -> none  [local(): key_piece.reshape(block_count, key_block, heads_here, head_size)]
    unnamed x10 -> x22, local copies, waits for them, and re-layouts: 62.5 us -> 61.3 us
  transfers between devices with their start and end apart: 5 -> 7, of which waited for: 3 -> 4; matrix products, arithmetic and copies ran while one was open for 44% -> 40% of each run, Pallas kernels for 0% -> 0%
where the time goes in v1:
time: 698 us; the launch traced here: 696 us
  waiting for transfers between devices  307 us (44%)
  matrix products  176 us (25%)
  other arithmetic  110 us (16%)
  local copies, waits for them, and re-layouts  85.9 us (12%)
  between operations  13.4 us (2%)
    ppermute x3, waiting for transfers between devices, around_the_ring(): lax.ppermute(held, axis, [(i, (i + 1) % devices) for i in range(devices)])  177 us
    reduce_scatter x1, waiting for transfers between devices, local(): lax.psum_scatter(jnp.dot(context, out_weight, preferred_element_type=jnp....  129 us
    unnamed x22, local copies, waits for them, and re-layouts  61.3 us
    dot_general x4, matrix products, step_block(): jnp.einsum('hqk,khd->hqd', exponent.astype(jnp.bfloat16), block_values, p...  53.8 us
    sin x1, other arithmetic, sincos_table(): jnp.sin(row_angle)  46.9 us
    dot_general x4, matrix products, step_block(): jnp.einsum('hqd,khd->hqk', query_heads, block_keys, preferred_element_typ...  46.4 us
    reduce_sum x4, other arithmetic, step_block(): new_total = run_total * rescale + jnp.sum(exponent, axis=2)  42.2 us
    dot_general x1, matrix products, local(): jnp.dot(flat_normed, qkv_matrix, preferred_element_type=jnp.float32)  36.4 us
  transfers between devices with their start and end apart: 7, of which 4 were waited for; matrix products, arithmetic and copies ran while one was open for 40% of the time, Pallas kernels for 0%

profile of v1, /device:TPU:0, one launch (start us, length us, event | category | flops | bytes accessed | tf_op | source)
XLA Modules:
  0.0 695.6 jit_solution(14699555758978112750)
XLA Ops:
  8.0 36.7 %copy.12 = bf16[6144,3,6,128]{0,3,2,1:T(8,128)(2,1)} copy(bf16[6144,3,6,128]{3,0,2,1:T(8,128)(2,1)} %param.13) | data formatting | bytes 56623104 | tf_op args[4]
  44.8 46.9 %multiply_sine_fusion.1 = (f32[1024,1536]{1,0:T(8,128)}, f32[1024,1536]{1,0:T(8,128)}, f32[1024,1536]{1,0:T(8,128)}, f32[1024,1536]{1,0:T(8,128)}) fusion(f32[1536]{0:T(1024)S(1)} %negate_power_fusion, f32[1024]{0:T(1024)S(1)} %get-tuple-element.118, f32[1024]{0:T(1024)S(1)} %get-tuple-element.117), kind=kLoop, calls=%fused_computation.35 | loop fusion | flops 3145728 | bytes 25180160 | tf_op jit(solution)/shard_map/sin | solution.py:26
  91.8 24.2 %fusion.29 = (f32[1024]{0:T(1024)S(1)}, f32[1024,6144]{1,0:T(8,128)}) fusion(f32[1024,1536]{1,0:T(8,128)} %get-tuple-element.111, f32[1024,1536]{1,0:T(8,128)} %get-tuple-element.112, f32[1024,1536]{1,0:T(8,128)} %get-tuple-element.108, f32[1024,1536]{1,0:T(8,128)} %get-tuple-element.107, f32[6144]{0:T(1024)S(1)} %convert_element_type.52, ...), kind=kOutput, calls=%fused_computation.69 | convolution fusion | flops 9701424128 | bytes 61370368 | tf_op jit(solution)/shard_map/dot_general | solution.py:53
  126.2 36.4 %fusion.19 = f32[1024,3,6,128]{0,3,2,1:T(8,128)S(1)} fusion(bf16[6144,3,6,128]{0,3,2,1:T(8,128)(2,1)} %copy.12, f32[1024,6144]{1,0:T(8,128)} %get-tuple-element.116, f32[6144]{0:T(1024)S(1)} %convert_element_type.57, f32[1024]{0:T(1024)S(1)} %add_rsqrt_fusion.2, f32[1024]{0:T(1024)S(1)} %broadcast_multiply_fusion.2), kind=kOutput, calls=%fused_computation.22 | convolution fusion | flops 29016195072 | bytes 62947328 | tf_op jit(solution)/shard_map/dot_general | solution.py:59
  180.8 61.9 %collective-permute-done = bf16[1024,6,128]{0,2,1:T(8,128)(2,1)S(1)} collective-permute-done((bf16[1024,6,128]{0,2,1:T(8,128)(2,1)S(1)}, bf16[1024,6,128]{0,2,1:T(8,128)(2,1)S(1)}, u32[]{:S(2)}, u32[]{:S(2)}) %collective-permute-start) | collective-permute-done | bytes 1572896 | tf_op jit(solution)/shard_map/ppermute | solution.py:14
  243.8 56.7 %collective-permute-done.1 = bf16[1024,6,128]{0,2,1:T(8,128)(2,1)} collective-permute-done((bf16[1024,6,128]{0,2,1:T(8,128)(2,1)S(1)}, bf16[1024,6,128]{0,2,1:T(8,128)(2,1)}, u32[]{:S(2)}, u32[]{:S(2)}) %collective-permute-start.1) | collective-permute-done | bytes 1572896 | tf_op jit(solution)/shard_map/ppermute | solution.py:14
  302.8 58.4 %collective-permute-done.2 = bf16[1024,6,128]{0,2,1:T(8,128)(2,1)} collective-permute-done((bf16[1024,6,128]{0,2,1:T(8,128)(2,1)}, bf16[1024,6,128]{0,2,1:T(8,128)(2,1)}, u32[]{:S(2)}, u32[]{:S(2)}) %collective-permute-start.2) | collective-permute-done | bytes 1572896 | tf_op jit(solution)/shard_map/ppermute | solution.py:14
  379.8 11.1 %reshape.82 = bf16[4,1024,6,128]{1,0,3,2:T(4,128)(2,1)} reshape(bf16[4096,1,6,128]{0,3,2,1:T(8,128)(2,1)} %all-gather.9.cloned.1.call-done) | data formatting | bytes 12582912 | tf_op jit(solution)/shard_map/reshape | solution.py:78
  390.9 11.2 %copy.18 = bf16[4,1024,6,128]{3,1,2,0:T(8,128)(2,1)} copy(bf16[4,1024,6,128]{1,0,3,2:T(4,128)(2,1)} %reshape.82) | data formatting | bytes 12582912
  402.1 142.5 %while.15 = (s32[]{:T(128)}, f32[6,1024]{1,0:T(8,128)S(1)}, f32[6,1024]{1,0:T(8,128)S(1)}, f32[6,1024,128]{2,1,0:T(8,128)}, bf16[4,1024,6,128]{3,1,0,2:T(8,128)(...) while((s32[]{:T(128)}, f32[6,1024]{1,0:T(8,128)S(1)}, ...), condition=%wide.region_9.10_spmd.clone, body=%wide.region_6.9_spmd.clone.sunk | while | flops 3273947136 | bytes 86901856 | solution.py:100
  402.1 11.6 %bitcast_reduce_fusion.2 = (f32[6,1024]{1,0:T(8,128)S(1)}, f32[6,1024,1024]{2,1,0:T(8,128)}) fusion(bf16[6,1024,128]{2,1,0:T(8,128)(2,1)S(1)} %get-tuple-element.195, bf16[4,1024,6,128]{3,1,0,2:T(8,128)(2,1)} %get-tuple-element.194, s32[]{:T(128)} %get-tuple-element.181), kind=kOutput, calls=%fused_computation.1.clone.1 | convolution fusion | flops 1623189504 | bytes 28336640 | tf_op jit(solution)/shard_map/while/body/eval_jaxpr/hqd,khd->hqk/dot_general | solution.py:84
  413.7 10.5 %fusion.43 = f32[6,1024]{1,0:T(8,128)S(1)} fusion(f32[6,1024,1024]{2,1,0:T(8,128)} %get-tuple-element.169, f32[6,1024]{1,0:T(8,128)S(1)} %select_maximum_fusion.2), kind=kLoop, calls=%fused_computation.4.clone.1 | loop fusion | flops 18868224 | bytes 25214976 | tf_op jit(solution)/shard_map/while/body/eval_jaxpr/reduce_sum | solution.py:90
  424.3 12.8 %fusion.45 = f32[6,1024,128]{2,1,0:T(8,128)} fusion(f32[6,1024,128]{2,1,0:T(8,128)} %get-tuple-element.184, f32[6,1024,1024]{2,1,0:T(8,128)} %get-tuple-element.169, f32[6,1024]{1,0:T(8,128)S(1)} %select_maximum_fusion.2, bf16[4,1024,6,128]{3,1,2,0:T(8,128)(2,1)} %get-tuple-element.196, s32[]{:T(128)} %get-tuple-element.181, ...), kind=kOutput, calls=%fused_computation.9.clone.1 | convolution fusion | flops 1631846400 | bytes 33079808 | tf_op jit(solution)/shard_map/while/body/eval_jaxpr/hqk,khd->hqd/dot_general | solution.py:91
  437.1 11.6 %bitcast_reduce_fusion.2 = (f32[6,1024]{1,0:T(8,128)S(1)}, f32[6,1024,1024]{2,1,0:T(8,128)}) fusion(bf16[6,1024,128]{2,1,0:T(8,128)(2,1)S(1)} %get-tuple-element.195, bf16[4,1024,6,128]{3,1,0,2:T(8,128)(2,1)} %get-tuple-element.194, s32[]{:T(128)} %get-tuple-element.181), kind=kOutput, calls=%fused_computation.1.clone.1 | convolution fusion | flops 1623189504 | bytes 28336640 | tf_op jit(solution)/shard_map/while/body/eval_jaxpr/hqd,khd->hqk/dot_general | solution.py:84
  448.7 10.5 %fusion.43 = f32[6,1024]{1,0:T(8,128)S(1)} fusion(f32[6,1024,1024]{2,1,0:T(8,128)} %get-tuple-element.169, f32[6,1024]{1,0:T(8,128)S(1)} %select_maximum_fusion.2), kind=kLoop, calls=%fused_computation.4.clone.1 | loop fusion | flops 18868224 | bytes 25214976 | tf_op jit(solution)/shard_map/while/body/eval_jaxpr/reduce_sum | solution.py:90
  459.3 13.7 %fusion.45 = f32[6,1024,128]{2,1,0:T(8,128)} fusion(f32[6,1024,128]{2,1,0:T(8,128)} %get-tuple-element.184, f32[6,1024,1024]{2,1,0:T(8,128)} %get-tuple-element.169, f32[6,1024]{1,0:T(8,128)S(1)} %select_maximum_fusion.2, bf16[4,1024,6,128]{3,1,2,0:T(8,128)(2,1)} %get-tuple-element.196, s32[]{:T(128)} %get-tuple-element.181, ...), kind=kOutput, calls=%fused_computation.9.clone.1 | convolution fusion | flops 1631846400 | bytes 33079808 | tf_op jit(solution)/shard_map/while/body/eval_jaxpr/hqk,khd->hqd/dot_general | solution.py:91
  472.9 11.6 %bitcast_reduce_fusion.2 = (f32[6,1024]{1,0:T(8,128)S(1)}, f32[6,1024,1024]{2,1,0:T(8,128)}) fusion(bf16[6,1024,128]{2,1,0:T(8,128)(2,1)S(1)} %get-tuple-element.195, bf16[4,1024,6,128]{3,1,0,2:T(8,128)(2,1)} %get-tuple-element.194, s32[]{:T(128)} %get-tuple-element.181), kind=kOutput, calls=%fused_computation.1.clone.1 | convolution fusion | flops 1623189504 | bytes 28336640 | tf_op jit(solution)/shard_map/while/body/eval_jaxpr/hqd,khd->hqk/dot_general | solution.py:84
  484.5 10.5 %fusion.43 = f32[6,1024]{1,0:T(8,128)S(1)} fusion(f32[6,1024,1024]{2,1,0:T(8,128)} %get-tuple-element.169, f32[6,1024]{1,0:T(8,128)S(1)} %select_maximum_fusion.2), kind=kLoop, calls=%fused_computation.4.clone.1 | loop fusion | flops 18868224 | bytes 25214976 | tf_op jit(solution)/shard_map/while/body/eval_jaxpr/reduce_sum | solution.py:90
  495.1 13.7 %fusion.45 = f32[6,1024,128]{2,1,0:T(8,128)} fusion(f32[6,1024,128]{2,1,0:T(8,128)} %get-tuple-element.184, f32[6,1024,1024]{2,1,0:T(8,128)} %get-tuple-element.169, f32[6,1024]{1,0:T(8,128)S(1)} %select_maximum_fusion.2, bf16[4,1024,6,128]{3,1,2,0:T(8,128)(2,1)} %get-tuple-element.196, s32[]{:T(128)} %get-tuple-element.181, ...), kind=kOutput, calls=%fused_computation.9.clone.1 | convolution fusion | flops 1631846400 | bytes 33079808 | tf_op jit(solution)/shard_map/while/body/eval_jaxpr/hqk,khd->hqd/dot_general | solution.py:91
  508.8 11.6 %bitcast_reduce_fusion.2 = (f32[6,1024]{1,0:T(8,128)S(1)}, f32[6,1024,1024]{2,1,0:T(8,128)}) fusion(bf16[6,1024,128]{2,1,0:T(8,128)(2,1)S(1)} %get-tuple-element.195, bf16[4,1024,6,128]{3,1,0,2:T(8,128)(2,1)} %get-tuple-element.194, s32[]{:T(128)} %get-tuple-element.181), kind=kOutput, calls=%fused_computation.1.clone.1 | convolution fusion | flops 1623189504 | bytes 28336640 | tf_op jit(solution)/shard_map/while/body/eval_jaxpr/hqd,khd->hqk/dot_general | solution.py:84
  520.4 10.5 %fusion.43 = f32[6,1024]{1,0:T(8,128)S(1)} fusion(f32[6,1024,1024]{2,1,0:T(8,128)} %get-tuple-element.169, f32[6,1024]{1,0:T(8,128)S(1)} %select_maximum_fusion.2), kind=kLoop, calls=%fused_computation.4.clone.1 | loop fusion | flops 18868224 | bytes 25214976 | tf_op jit(solution)/shard_map/while/body/eval_jaxpr/reduce_sum | solution.py:90
  531.0 13.7 %fusion.45 = f32[6,1024,128]{2,1,0:T(8,128)} fusion(f32[6,1024,128]{2,1,0:T(8,128)} %get-tuple-element.184, f32[6,1024,1024]{2,1,0:T(8,128)} %get-tuple-element.169, f32[6,1024]{1,0:T(8,128)S(1)} %select_maximum_fusion.2, bf16[4,1024,6,128]{3,1,2,0:T(8,128)(2,1)} %get-tuple-element.196, s32[]{:T(128)} %get-tuple-element.181, ...), kind=kOutput, calls=%fused_computation.9.clone.1 | convolution fusion | flops 1631846400 | bytes 33079808 | tf_op jit(solution)/shard_map/while/body/eval_jaxpr/hqk,khd->hqd/dot_general | solution.py:91
  544.6 15.3 %bitcast_convert_fusion = bf16[1024,6144]{1,0:T(8,128)(2,1)} fusion(bf16[6,128,6144]{2,1,0:T(8,128)(2,1)} %all-gather.7.cloned.1.call-done, f32[6,1024,128]{2,1,0:T(8,128)} %get-tuple-element.43, f32[6,1024]{1,0:T(8,128)S(1)} %get-tuple-element.44), kind=kOutput, calls=%fused_computation.25 | convolution fusion | flops 9671540736 | bytes 25190400 | tf_op jit(solution)/shard_map/dot_general | solution.py:108
  560.0 129.1 %reduce-scatter.2.cloned.1.call-done = bf16[128,6144]{1,0:T(8,128)(2,1)} async-done(((bf16[1024,6144]{1,0:T(8,128)(2,1)}), bf16[128,6144]{1,0:T(8,128)(2,1)}) %reduce-scatter.2.cloned.1.call-update) | async-done | bytes 1572880 | tf_op jit(solution)/shard_map/reduce_scatter | solution.py:107
  (69 shorter events, 51.8 us)
Async XLA Ops:
  6.5 85.2 %all-gather.5.cloned.1.call-start = ((), (), s32[]{:S(2)}) async-start(), calls=%async_computation.1 | async-start | bytes 1769472 | tf_op jit(solution)/shard_map/all_gather | solution.py:48
  7.3 372.6 %all-gather.9.cloned.1.call-start = ((), (), s32[]{:S(2)}) async-start(), calls=%async_computation.4 | async-start | bytes 7864320 | tf_op jit(solution)/shard_map/all_gather | solution.py:73
  8.0 36.7 %copy-start.4 = (bf16[6144]{0:T(1024)(128)(2,1)S(1)}, bf16[6144]{0:T(1024)(128)(2,1)}, u32[]{:S(2)}) copy-start(bf16[6144]{0:T(1024)(128)(2,1)} %param.12) | copy-start | bytes 36868
  126.2 41.6 %copy-start.5 = (f32[2,6,128]{2,0,1:T(2,128)S(1)}, f32[2,6,128]{2,0,1:T(2,128)}, u32[]{:S(2)}) copy-start(f32[2,6,128]{2,0,1:T(2,128)} %param.14) | copy-start | bytes 18436
  162.6 3.6 copy-start
  167.7 377.0 %all-gather.7.cloned.1.call-start = ((), (), s32[]{:S(2)}) async-start(), calls=%async_computation.2 | async-start | bytes 11796480 | tf_op jit(solution)/shard_map/all_gather | solution.py:104
  167.7 8.1 %copy-start.1 = (f32[1024,3,6,128]{0,3,2,1:T(8,128)S(1)}, f32[1024,3,6,128]{0,3,2,1:T(8,128)}, u32[]{:S(2)}) copy-start(f32[1024,3,6,128]{0,3,2,1:T(8,128)} %copy-done) | copy-start | bytes 28311556
  177.8 64.9 %collective-permute-start = (bf16[1024,6,128]{0,2,1:T(8,128)(2,1)S(1)}, bf16[1024,6,128]{0,2,1:T(8,128)(2,1)S(1)}, u32[]{:S(2)}, u32[]{:S(2)}) collective-permute-start(bf16[1024,6,128]{0,2,1:T(8,128)(2,1)S(1)} %get-tuple-element.106), channel_id=1, source_target_pairs={{0,8},{8,16},{16,24},{24,0},{1,9},{9,17},{17,25},{25,1},{2,10},{10... | collective-permute-start | bytes 4718600 | tf_op jit(solution)/shard_map/ppermute | solution.py:14
  242.7 1.1 copy-start.2
  243.8 56.7 %collective-permute-start.1 = (bf16[1024,6,128]{0,2,1:T(8,128)(2,1)S(1)}, bf16[1024,6,128]{0,2,1:T(8,128)(2,1)}, u32[]{:S(2)}, u32[]{:S(2)}) collective-permute-start(bf16[1024,6,128]{0,2,1:T(8,128)(2,1)S(1)} %collective-permute-done), channel_id=1, source_target_pairs={{0,8},{8,16},{16,24},{24,0},{1,9},{9,17},{17,25},{25,1},{2,10},{10... | collective-permute-start | bytes 4718600 | tf_op jit(solution)/shard_map/ppermute | solution.py:14
  300.5 60.7 %collective-permute-start.2 = (bf16[1024,6,128]{0,2,1:T(8,128)(2,1)}, bf16[1024,6,128]{0,2,1:T(8,128)(2,1)}, u32[]{:S(2)}, u32[]{:S(2)}) collective-permute-start(bf16[1024,6,128]{0,2,1:T(8,128)(2,1)} %collective-permute-done.1), channel_id=1, source_target_pairs={{0,8},{8,16},{16,24},{24,0},{1,9},{9,17},{17,25},{25,1},{2,10},{10... | collective-permute-start | bytes 4718600 | tf_op jit(solution)/shard_map/ppermute | solution.py:14
  300.5 388.6 %reduce-scatter.2.cloned.1.call-start = ((), (), s32[]{:S(2)}) async-start(), calls=%async_computation.3 | async-start | bytes 14155776 | tf_op jit(solution)/shard_map/reduce_scatter | solution.py:107
  302.8 61.5 %copy-start.3 = (bf16[1024,6,128]{0,2,1:T(8,128)(2,1)S(1)}, bf16[1024,6,128]{0,2,1:T(8,128)(2,1)}, u32[]{:S(2)}) copy-start(bf16[1024,6,128]{0,2,1:T(8,128)(2,1)} %copy-done.2) | copy-start | bytes 4718596
Sparse Core Ops, SparseCore 0:
  8.9 27.9 all-gather.4
  167.8 118.7 all-gather.8
  300.7 119.6 all-gather.6
  560.1 128.9 reduce-scatter.1
